TPU v7x, 128 devices: a whole 4x4x4 slice. The times are simulated.
128 devices in a mesh: grp: 8 (over z, y_lo), slab: 16 (over y_hi, x, core).
Axes of the slice: x: 4, y: 4 (y_hi: 2, y_lo: 2; y = y_hi * 2 + y_lo), z: 4, core: 2. Of those that a mesh axis runs over, the one named last changes fastest.
Arguments:
- orbitals: float32 [16, 96, 9216], P('grp', 'slab'), may hold values from -6 to 6
- occupation: int32 [16], P('grp'), may hold values from 1 to 4
- kernel_hat: float32 [192, 36864], P('slab'), may hold values from 0.02 to 1200, as said below
- pair_mask: int32 [1], replicated, may hold values from 1 to 7
Outputs:
- exchange_terms: float32 [16, 96, 9216], P('grp', 'slab')
Inputs may be any that keep to these rules, and one draw needn't show every extreme that they name: In this round group g is paired with group g XOR pair_mask. kernel_hat is positive, and unchanged when each frequency index k is replaced by (192 - k) mod 192 in all three dimensions at once.
All inputs are finite; a program needn't handle non-finite values.
Results may differ from a plain program's by a relative error of at most 0.0001.
Values sent between devices are 32-bit elements; how exact they have to be, the bound alone decides.
A program may use at most 64 MiB of HBM per device.

v0:
```python
import math

import jax
import jax.numpy as jnp
from jax import lax
from jax.sharding import PartitionSpec as P

G = 96


def swapped(value, axis, apart):
    mask = 2**apart
    pairs = [(source, source ^ mask) for source in range(lax.axis_size(axis))]
    return lax.ppermute(value, axis, pairs)


def dft_tables(size_in, size_out, period):
    row_index = lax.broadcasted_iota(jnp.int32, (size_in, size_out), 0)
    col_index = lax.broadcasted_iota(jnp.int32, (size_in, size_out), 1)
    phase_angle = (row_index * col_index % period).astype(jnp.float32) * (2.0 * math.pi / period)
    return (jnp.cos(phase_angle), jnp.sin(phase_angle))


def contract(form, left, right):
    return jnp.einsum(
        form, left, right, precision=lax.Precision.HIGHEST, preferred_element_type=jnp.float32
    )


def local(orbitals, occupation, kernel_hat, pair_mask):
    orbit_count = orbitals.shape[0]
    half_count = orbit_count // 2
    plane_count = orbitals.shape[1]
    grid_len = G
    padded_len = 2 * G
    kernel_cube = kernel_hat.reshape(kernel_hat.shape[0], padded_len, padded_len)
    cos_fwd, sin_fwd = dft_tables(grid_len, padded_len, padded_len)
    cos_inv, sin_inv = dft_tables(padded_len, grid_len, padded_len)
    cos_inv = cos_inv / padded_len
    sin_inv = sin_inv / padded_len
    forward_pair = jnp.stack([jnp.stack([cos_fwd, -sin_fwd]), jnp.stack([sin_fwd, cos_fwd])])
    inverse_pair = jnp.stack([jnp.stack([cos_inv, sin_inv]), jnp.stack([-sin_inv, cos_inv])])

    def line_work(pencils):
        y_spectra = contract("nckxy,cdyl->ndkxl", pencils, forward_pair)
        spectra = contract("nckxl,cdxm->ndklm", y_spectra, forward_pair)
        spectra = spectra * kernel_cube[None, None]
        x_back = contract("ncklm,cdmx->ndklx", spectra, inverse_pair)
        return contract("ncklx,cdly->ndkxy", x_back, inverse_pair)

    def packed_potential(density_pair):
        spread = contract("ncxyz,cdzk->ndkxy", density_pair, forward_pair)
        planes = lax.all_to_all(
            line_work(lax.all_to_all(spread, "slab", split_axis=2, concat_axis=3, tiled=True)),
            "slab",
            split_axis=3,
            concat_axis=2,
            tiled=True,
        )
        return contract("nckxy,cdkz->ndxyz", planes, inverse_pair)

    pair_bits = pair_mask[0]
    own_group = lax.axis_index("grp")
    partner_group = jnp.bitwise_xor(own_group, pair_bits)
    upper_side = (own_group > partner_group).astype(jnp.int32)
    weights = 0.25 * occupation.astype(jnp.float32)
    level_count = lax.axis_size("grp").bit_length() - 1
    theirs = orbitals
    their_weights = weights
    for bit_level in range(level_count):
        arrived = swapped((theirs, their_weights), "grp", bit_level)
        chosen_flag = jnp.bitwise_and(jnp.right_shift(pair_bits, bit_level), 1) == 1
        theirs = jnp.where(chosen_flag, arrived[0], theirs)
        their_weights = jnp.where(chosen_flag, arrived[1], their_weights)
    paired = theirs.reshape(half_count, 2, plane_count, grid_len * grid_len)
    paired_weights = their_weights.reshape(half_count, 2)

    def add_returned(returned, parity, term):
        current = lax.dynamic_slice_in_dim(returned, parity, 1, 1)
        return lax.dynamic_update_slice_in_dim(returned, current + term[:, None], parity, 1)

    def twin_step(pair_number, loop_state):
        kept_rows, returned = loop_state
        first_row = 2 * pair_number
        second_row = first_row + 1
        own_first = lax.dynamic_index_in_dim(orbitals, first_row, 0, keepdims=False)
        own_second = lax.dynamic_index_in_dim(orbitals, second_row, 0, keepdims=False)
        weight_first = lax.dynamic_index_in_dim(weights, first_row, 0, keepdims=False)
        weight_second = lax.dynamic_index_in_dim(weights, second_row, 0, keepdims=False)
        parity_first = upper_side % 2
        parity_second = 1 - parity_first
        chosen_first = lax.dynamic_index_in_dim(paired, parity_first, 1, keepdims=False)
        chosen_second = lax.dynamic_index_in_dim(paired, parity_second, 1, keepdims=False)
        cweight_first = lax.dynamic_index_in_dim(paired_weights, parity_first, 1, keepdims=False)
        cweight_second = lax.dynamic_index_in_dim(paired_weights, parity_second, 1, keepdims=False)
        density_pair = jnp.stack(
            [own_first[None] * chosen_first, own_second[None] * chosen_second], axis=1
        )
        density_pair = density_pair.reshape(half_count, 2, plane_count, grid_len, grid_len)
        fields = packed_potential(density_pair).reshape(
            half_count, 2, plane_count, grid_len * grid_len
        )
        field_first = fields[:, 0]
        field_second = fields[:, 1]
        kept_first = -jnp.sum(cweight_first[:, None, None] * field_first * chosen_first, axis=0)
        kept_second = -jnp.sum(cweight_second[:, None, None] * field_second * chosen_second, axis=0)
        kept_rows = lax.dynamic_update_index_in_dim(kept_rows, kept_first, first_row, 0)
        kept_rows = lax.dynamic_update_index_in_dim(kept_rows, kept_second, second_row, 0)
        returned = add_returned(
            returned, parity_first, -weight_first * field_first * own_first[None]
        )
        returned = add_returned(
            returned, parity_second, -weight_second * field_second * own_second[None]
        )
        return (kept_rows, returned)

    kept_start = jnp.zeros(orbitals.shape, jnp.float32)
    returned_start = jnp.zeros((half_count, 2, plane_count, grid_len * grid_len), jnp.float32)
    kept_rows, returned = lax.fori_loop(0, half_count, twin_step, (kept_start, returned_start))
    outgoing = returned.reshape(orbit_count, plane_count, grid_len * grid_len)
    incoming = outgoing
    for bit_level in range(level_count):
        arrived_terms = swapped(incoming, "grp", bit_level)
        chosen_flag = jnp.bitwise_and(jnp.right_shift(pair_bits, bit_level), 1) == 1
        incoming = jnp.where(chosen_flag, arrived_terms, incoming)
    return kept_rows + incoming


def solution(mesh):
    return jax.shard_map(
        local,
        mesh=mesh,
        in_specs=(P("grp", "slab", None), P("grp"), P("slab", None), P()),
        out_specs=P("grp", "slab", None),
        check_vma=False,
    )
```

profile of v0, /device:TPU:6, one launch (start us, length us, event | category | flops | bytes accessed | tf_op | source)
XLA Modules:
  0.0 154.5 jit_solution(10319154145023232211)
XLA Ops:
  0.0 1.6 %collective-permute-start.3 = (f32[2,6,9216]{2,0,1:T(2,128)}, f32[2,6,9216]{2,0,1:T(2,128)S(1)}, u32[]{:S(2)}, u32[]{:S(2)}) collective-permute-start(f32[2,6,9216]{2,0,1:T(2,128)} %param.4), channel_id=1, source_target_pairs={{0,16},{16,0},{32,48},{48,32},{64,80},{80,64},{96,112},{112,96},{1... | collective-permute-start | bytes 1327112 | tf_op jit(solution)/shard_map/ppermute | solution.py:14
  2.2 9.9 %collective-permute-done.3 = f32[2,6,9216]{2,0,1:T(2,128)S(1)} collective-permute-done((f32[2,6,9216]{2,0,1:T(2,128)}, f32[2,6,9216]{2,0,1:T(2,128)S(1)}, u32[]{:S(2)}, u32[]{:S(2)}) %collective-permute-start.3) | collective-permute-done | bytes 442400 | tf_op jit(solution)/shard_map/ppermute | solution.py:14
  12.4 2.0 %collective-permute-start.4 = (f32[2,6,9216]{2,0,1:T(2,128)S(1)}, f32[2,6,9216]{2,0,1:T(2,128)S(1)}, u32[]{:S(2)}, u32[]{:S(2)}) collective-permute-start(f32[2,6,9216]{2,0,1:T(2,128)S(1)} %broadcast_select_fusion.1), channel_id=1, source_target_pairs={{0,32},{16,48},{32,0},{48,16},{64,96},{80,112},{96,64},{112,80},{1... | collective-permute-start | bytes 1327112 | tf_op jit(solution)/shard_map/ppermute | solution.py:14
  14.4 9.3 %collective-permute-done.4 = f32[2,6,9216]{2,0,1:T(2,128)S(1)} collective-permute-done((f32[2,6,9216]{2,0,1:T(2,128)S(1)}, f32[2,6,9216]{2,0,1:T(2,128)S(1)}, u32[]{:S(2)}, u32[]{:S(2)}) %collective-permute-start.4) | collective-permute-done | bytes 442400 | tf_op jit(solution)/shard_map/ppermute | solution.py:14
  23.9 3.8 %collective-permute-start.5 = (f32[2,6,9216]{2,0,1:T(2,128)S(1)}, f32[2,6,9216]{2,0,1:T(2,128)S(1)}, u32[]{:S(2)}, u32[]{:S(2)}) collective-permute-start(f32[2,6,9216]{2,0,1:T(2,128)S(1)} %broadcast_select_fusion.3), channel_id=1, source_target_pairs={{0,64},{16,80},{32,96},{48,112},{64,0},{80,16},{96,32},{112,48},{1... | collective-permute-start | bytes 1327112 | tf_op jit(solution)/shard_map/ppermute | solution.py:14
  28.6 7.9 %collective-permute-done.5 = f32[2,6,9216]{2,0,1:T(2,128)S(1)} collective-permute-done((f32[2,6,9216]{2,0,1:T(2,128)S(1)}, f32[2,6,9216]{2,0,1:T(2,128)S(1)}, u32[]{:S(2)}, u32[]{:S(2)}) %collective-permute-start.5) | collective-permute-done | bytes 442400 | tf_op jit(solution)/shard_map/ppermute | solution.py:14
  36.7 1.4 multiply_reduce_fusion.1
  38.4 1.2 convolution_bitcast_fusion
  39.6 1.9 %copy.50 = f32[1,2,192,6,96]{4,1,3,0,2:T(2,128)} copy(f32[1,2,192,6,96]{4,2,3,1,0:T(8,128)S(1)} %convolution_bitcast_fusion) | data formatting | bytes 1769472 | tf_op jit(solution)/shard_map/while/body/eval_jaxpr/ncxyz,cdzk->ndkxy/transpose | solution.py:25
  41.5 7.4 %all-to-all-start = ((f32[1,2,192,6,96]{4,1,3,0,2:T(2,128)}), f32[1,2,192,6,96]{4,1,3,0,2:T(2,128)S(1)}, u32[]{:S(2)}, u32[]{:S(2)}) async-start(f32[1,2,192,6,96]{4,1,3,0,2:T(2,128)} %copy.50), calls=%async_computation | async-start | bytes 2359296 | tf_op jit(solution)/shard_map/while/body/eval_jaxpr/all_to_all | solution.py:54
  49.0 2.3 %mul.246 = f32[12,192,192]{2,1,0:T(8,128)S(1)} reshape(f32[12,36864]{1,0:T(8,128)} %param.6) | data formatting | bytes 3538944 | tf_op jit(solution)/shard_map/while/body/eval_jaxpr/mul | solution.py:47
  51.3 2.1 %copy.54 = f32[12,192,192]{1,2,0:T(8,128)} copy(f32[12,192,192]{2,1,0:T(8,128)S(1)} %mul.246) | data formatting | bytes 3538944 | tf_op jit(solution)/shard_map/while/body/eval_jaxpr/mul | solution.py:47
  54.3 10.6 %all-to-all-done = f32[1,2,192,6,96]{4,1,3,0,2:T(2,128)S(1)} async-done(((f32[1,2,192,6,96]{4,1,3,0,2:T(2,128)}), f32[1,2,192,6,96]{4,1,3,0,2:T(2,128)S(1)}, u32[]{:S(2)}, u32[]{:S(2)}) %all-to-all-start) | async-done | bytes 884768 | tf_op jit(solution)/shard_map/while/body/eval_jaxpr/all_to_all | solution.py:54
  65.5 2.1 %fusion.12 = f32[2,192,12,96,1]{3,1,4,2,0:T(8,128)S(1)} fusion(f32[2,12,96,96]{3,0,2,1:T(2,128)S(1)} %bitcast.166, f32[1,2,96,192]{2,3,0,1:T(8,128)S(1)} %copy-done.8, f32[1,2,96,192]{2,3,0,1:T(8,128)S(1)} %copy-done.6), kind=kOutput, calls=%fused_computation.12 | convolution fusion | flops 1019289600 | bytes 2949120 | tf_op jit(solution)/shard_map/while/body/eval_jaxpr/nckxy,cdyl->ndkxl/dot_general | solution.py:25
  67.6 3.9 %fusion.5 = f32[2,192,12,192,1]{3,1,2,4,0:T(8,128)S(1)} fusion(f32[2,192,12,96,1]{3,1,4,2,0:T(8,128)S(1)} %fusion.12, f32[1,2,96,192]{2,3,0,1:T(8,128)S(1)} %copy-done.8, f32[1,2,96,192]{2,3,0,1:T(8,128)S(1)} %copy-done.6), kind=kOutput, calls=%fused_computation.5 | convolution fusion | flops 2038505472 | bytes 5603328 | tf_op jit(solution)/shard_map/while/body/eval_jaxpr/nckxl,cdxm->ndklm/dot_general | solution.py:25
  71.5 4.0 %fusion.1 = f32[2,96,12,192,1]{3,1,2,4,0:T(8,128)S(1)} fusion(f32[2,192,12,192,1]{3,1,2,4,0:T(8,128)S(1)} %fusion.5, f32[12,192,192]{1,2,0:T(8,128)S(1)} %copy-done, f32[1,2,192,96]{2,3,0,1:T(8,128)S(1)} %get-tuple-element.32, f32[1,2,192,96]{2,3,0,1:T(8,128)S(1)} %get-tuple-element.31), kind=kOutput, calls=%fused_computation.2 | convolution fusion | flops 2039390208 | bytes 7372800 | tf_op jit(solution)/shard_map/while/body/eval_jaxpr/ncklm,cdmx->ndklx/dot_general | solution.py:25
  75.6 3.0 %fusion.8 = f32[1,2,12,96,96]{3,4,2,1,0:T(8,128)S(1)} fusion(f32[2,96,12,192,1]{3,1,2,4,0:T(8,128)S(1)} %fusion.1, f32[1,2,192,96]{2,3,0,1:T(8,128)S(1)} %get-tuple-element.32, f32[1,2,192,96]{2,3,0,1:T(8,128)S(1)} %get-tuple-element.31), kind=kOutput, calls=%fused_computation.8 | convolution fusion | flops 1019289600 | bytes 2949120 | tf_op jit(solution)/shard_map/while/body/eval_jaxpr/ncklx,cdly->ndkxy/dot_general | solution.py:25
  78.5 1.4 copy.57
  79.9 7.0 %all-to-all-start.1 = ((f32[1,2,12,96,96]{4,1,2,0,3:T(2,128)}), f32[1,2,12,96,96]{4,1,2,0,3:T(2,128)S(1)}, u32[]{:S(2)}, u32[]{:S(2)}) async-start(f32[1,2,12,96,96]{4,1,2,0,3:T(2,128)} %copy.57), calls=%async_computation.1 | async-start | bytes 2359296 | tf_op jit(solution)/shard_map/while/body/eval_jaxpr/all_to_all | solution.py:53
  88.8 14.1 %all-to-all-done.1 = f32[1,2,12,96,96]{4,1,2,0,3:T(2,128)S(1)} async-done(((f32[1,2,12,96,96]{4,1,2,0,3:T(2,128)}), f32[1,2,12,96,96]{4,1,2,0,3:T(2,128)S(1)}, u32[]{:S(2)}, u32[]{:S(2)}) %all-to-all-start.1) | async-done | bytes 884768 | tf_op jit(solution)/shard_map/while/body/eval_jaxpr/all_to_all | solution.py:53
  103.9 1.2 convolution_bitcast_fusion.1
  107.2 4.7 %dynamic_update_slice.18 = f32[2,6,9216]{2,0,1:T(2,128)S(1)} dynamic-update-slice(f32[2,6,9216]{2,0,1:T(2,128)S(1)} %bitcast.167, f32[1,6,9216]{2,0,1:T(1,128)S(1)} %fusion.24, s32[]{:T(128)S(6)} %select_n.158, s32[]{:T(128)} %constant.85.clone.1, s32[]{:T(128)} %constant.85.clone.1) | dynamic-update-slice | bytes 442372 | tf_op jit(solution)/shard_map/while/body/eval_jaxpr/dynamic_update_slice | solution.py:80
  112.6 1.4 collective-permute-start
  114.0 11.1 %collective-permute-done = f32[2]{0:T(128)S(1)} collective-permute-done((f32[2]{0:T(128)S(1)}, f32[2]{0:T(128)S(1)}, u32[]{:S(2)}, u32[]{:S(2)}) %collective-permute-start) | collective-permute-done | bytes 40 | tf_op jit(solution)/shard_map/ppermute | solution.py:14
  126.2 1.1 collective-permute-start.7
  127.4 1.2 collective-permute-done.1
  128.6 2.9 %collective-permute-start.2 = (f32[2]{0:T(128)S(1)}, f32[2]{0:T(128)S(1)}, u32[]{:S(2)}, u32[]{:S(2)}) collective-permute-start(f32[2]{0:T(128)S(1)} %broadcast_select_fusion.6), channel_id=1, source_target_pairs={{0,64},{16,80},{32,96},{48,112},{64,0},{80,16},{96,32},{112,48},{1... | collective-permute-start | bytes 32 | tf_op jit(solution)/shard_map/ppermute | solution.py:14
  131.5 8.5 %collective-permute-done.2 = f32[2]{0:T(128)S(1)} collective-permute-done((f32[2]{0:T(128)S(1)}, f32[2]{0:T(128)S(1)}, u32[]{:S(2)}, u32[]{:S(2)}) %collective-permute-start.2) | collective-permute-done | bytes 40 | tf_op jit(solution)/shard_map/ppermute | solution.py:14
  141.0 1.0 collective-permute-start.8
  142.0 1.9 %fusion.26 = (f32[1,6,9216]{2,0,1:T(1,128)S(1)}, f32[1,6,9216]{2,0,1:T(1,128)S(1)}) fusion(f32[1,2,6,9216]{3,1,2,0:T(2,128)S(1)} %reshape.235, f32[2,6,9216]{2,0,1:T(2,128)S(1)} %copy-done.4, s32[]{:T(128)S(6)} %select_n.149, f32[]{:T(128)} %bitcast.1, s32[]{:T(128)S(6)} %select_n.158, f32[]{:T(128)} %bitcast.54), kind=kLoop, calls=%fused_computation.44 | loop fusion | flops 331776 | bytes 1327120 | tf_op jit(solution)/shard_map/while/body/eval_jaxpr/neg | solution.py:105
  143.9 9.2 %collective-permute-done.8 = f32[2,6,9216]{2,0,1:T(2,128)S(1)} collective-permute-done((f32[2,6,9216]{2,0,1:T(2,128)S(1)}, f32[2,6,9216]{2,0,1:T(2,128)S(1)}, u32[]{:S(2)}, u32[]{:S(2)}) %collective-permute-start.8) | collective-permute-done | bytes 442400 | tf_op jit(solution)/shard_map/ppermute | solution.py:14
  153.2 1.3 maximum_add_fusion
  (52 shorter events, 9.7 us)
Async XLA Ops:
  0.0 12.1 %collective-permute-start.3 = (f32[2,6,9216]{2,0,1:T(2,128)}, f32[2,6,9216]{2,0,1:T(2,128)S(1)}, u32[]{:S(2)}, u32[]{:S(2)}) collective-permute-start(f32[2,6,9216]{2,0,1:T(2,128)} %param.4), channel_id=1, source_target_pairs={{0,16},{16,0},{32,48},{48,32},{64,80},{80,64},{96,112},{112,96},{1... | collective-permute-start | bytes 1327112 | tf_op jit(solution)/shard_map/ppermute | solution.py:14
  2.2 34.4 %copy-start.1 = (f32[2,6,9216]{2,0,1:T(2,128)S(1)}, f32[2,6,9216]{2,0,1:T(2,128)}, u32[]{:S(2)}) copy-start(f32[2,6,9216]{2,0,1:T(2,128)} %param.4) | copy-start | bytes 1327108
  12.4 11.3 %collective-permute-start.4 = (f32[2,6,9216]{2,0,1:T(2,128)S(1)}, f32[2,6,9216]{2,0,1:T(2,128)S(1)}, u32[]{:S(2)}, u32[]{:S(2)}) collective-permute-start(f32[2,6,9216]{2,0,1:T(2,128)S(1)} %broadcast_select_fusion.1), channel_id=1, source_target_pairs={{0,32},{16,48},{32,0},{48,16},{64,96},{80,112},{96,64},{112,80},{1... | collective-permute-start | bytes 1327112 | tf_op jit(solution)/shard_map/ppermute | solution.py:14
  23.9 12.5 %collective-permute-start.5 = (f32[2,6,9216]{2,0,1:T(2,128)S(1)}, f32[2,6,9216]{2,0,1:T(2,128)S(1)}, u32[]{:S(2)}, u32[]{:S(2)}) collective-permute-start(f32[2,6,9216]{2,0,1:T(2,128)S(1)} %broadcast_select_fusion.3), channel_id=1, source_target_pairs={{0,64},{16,80},{32,96},{48,112},{64,0},{80,16},{96,32},{112,48},{1... | collective-permute-start | bytes 1327112 | tf_op jit(solution)/shard_map/ppermute | solution.py:14
  28.5 11.1 %copy-start.5 = (f32[1,2,96,192]{2,3,0,1:T(8,128)}, f32[1,2,96,192]{2,3,0,1:T(8,128)S(1)}, u32[]{:S(2)}) copy-start(f32[1,2,96,192]{2,3,0,1:T(8,128)S(1)} %get-tuple-element.33) | copy-start | bytes 442372
  28.5 11.1 %copy-start.7 = (f32[1,2,96,192]{2,3,0,1:T(8,128)}, f32[1,2,96,192]{2,3,0,1:T(8,128)S(1)}, u32[]{:S(2)}) copy-start(f32[1,2,96,192]{2,3,0,1:T(8,128)S(1)} %get-tuple-element.34) | copy-start | bytes 442372
  36.7 1.5 copy-start.3
  41.5 23.3 %all-to-all-start = ((f32[1,2,192,6,96]{4,1,3,0,2:T(2,128)}), f32[1,2,192,6,96]{4,1,3,0,2:T(2,128)S(1)}, u32[]{:S(2)}, u32[]{:S(2)}) async-start(f32[1,2,192,6,96]{4,1,3,0,2:T(2,128)} %copy.50), calls=%async_computation | async-start | bytes 2359296 | tf_op jit(solution)/shard_map/while/body/eval_jaxpr/all_to_all | solution.py:54
  53.4 12.0 %copy-start.6 = (f32[1,2,96,192]{2,3,0,1:T(8,128)S(1)}, f32[1,2,96,192]{2,3,0,1:T(8,128)}, u32[]{:S(2)}) copy-start(f32[1,2,96,192]{2,3,0,1:T(8,128)} %copy-done.5) | copy-start | bytes 442372
  53.4 12.0 %copy-start.8 = (f32[1,2,96,192]{2,3,0,1:T(8,128)S(1)}, f32[1,2,96,192]{2,3,0,1:T(8,128)}, u32[]{:S(2)}) copy-start(f32[1,2,96,192]{2,3,0,1:T(8,128)} %copy-done.7) | copy-start | bytes 442372
  67.6 3.9 %copy-start = (f32[12,192,192]{1,2,0:T(8,128)S(1)}, f32[12,192,192]{1,2,0:T(8,128)}, u32[]{:S(2)}) copy-start(f32[12,192,192]{1,2,0:T(8,128)} %copy.54) | copy-start | bytes 5308420
  78.5 8.5 %copy-start.9 = (s32[2]{0:T(128)S(1)}, s32[2]{0:T(128)}, u32[]{:S(2)}) copy-start(s32[2]{0:T(128)} %param.5) | copy-start | bytes 28
  79.9 23.0 %all-to-all-start.1 = ((f32[1,2,12,96,96]{4,1,2,0,3:T(2,128)}), f32[1,2,12,96,96]{4,1,2,0,3:T(2,128)S(1)}, u32[]{:S(2)}, u32[]{:S(2)}) async-start(f32[1,2,12,96,96]{4,1,2,0,3:T(2,128)} %copy.57), calls=%async_computation.1 | async-start | bytes 2359296 | tf_op jit(solution)/shard_map/while/body/eval_jaxpr/all_to_all | solution.py:53
  103.9 2.3 %copy-start.2 = (f32[2,6,9216]{2,0,1:T(2,128)S(1)}, f32[2,6,9216]{2,0,1:T(2,128)}, u32[]{:S(2)}) copy-start(f32[2,6,9216]{2,0,1:T(2,128)} %param.4) | copy-start | bytes 1327108
  106.4 35.6 %copy-start.4 = (f32[2,6,9216]{2,0,1:T(2,128)S(1)}, f32[2,6,9216]{2,0,1:T(2,128)}, u32[]{:S(2)}) copy-start(f32[2,6,9216]{2,0,1:T(2,128)} %copy-done.3) | copy-start | bytes 1327108
  111.9 14.1 %collective-permute-start.6 = (f32[2,6,9216]{2,0,1:T(2,128)S(1)}, f32[2,6,9216]{2,0,1:T(2,128)S(1)}, u32[]{:S(2)}, u32[]{:S(2)}) collective-permute-start(f32[2,6,9216]{2,0,1:T(2,128)S(1)} %dynamic_update_slice.18), channel_id=1, source_target_pairs={{0,16},{16,0},{32,48},{48,32},{64,80},{80,64},{96,112},{112,96},{1... | collective-permute-start | bytes 1327112 | tf_op jit(solution)/shard_map/ppermute | solution.py:14
  112.6 12.4 %collective-permute-start = (f32[2]{0:T(128)S(1)}, f32[2]{0:T(128)S(1)}, u32[]{:S(2)}, u32[]{:S(2)}) collective-permute-start(f32[2]{0:T(128)S(1)} %convert_multiply_fusion), channel_id=1, source_target_pairs={{0,16},{16,0},{32,48},{48,32},{64,80},{80,64},{96,112},{112,96},{1... | collective-permute-start | bytes 32 | tf_op jit(solution)/shard_map/ppermute | solution.py:14
  125.0 3.6 %collective-permute-start.1 = (f32[2]{0:T(128)S(1)}, f32[2]{0:T(128)S(1)}, u32[]{:S(2)}, u32[]{:S(2)}) collective-permute-start(f32[2]{0:T(128)S(1)} %broadcast_select_fusion.5), channel_id=1, source_target_pairs={{0,32},{16,48},{32,0},{48,16},{64,96},{80,112},{96,64},{112,80},{1... | collective-permute-start | bytes 32 | tf_op jit(solution)/shard_map/ppermute | solution.py:14
  126.2 14.5 %collective-permute-start.7 = (f32[2,6,9216]{2,0,1:T(2,128)S(1)}, f32[2,6,9216]{2,0,1:T(2,128)S(1)}, u32[]{:S(2)}, u32[]{:S(2)}) collective-permute-start(f32[2,6,9216]{2,0,1:T(2,128)S(1)} %broadcast_select_fusion), channel_id=1, source_target_pairs={{0,32},{16,48},{32,0},{48,16},{64,96},{80,112},{96,64},{112,80},{1... | collective-permute-start | bytes 1327112 | tf_op jit(solution)/shard_map/ppermute | solution.py:14
  128.6 11.5 %collective-permute-start.2 = (f32[2]{0:T(128)S(1)}, f32[2]{0:T(128)S(1)}, u32[]{:S(2)}, u32[]{:S(2)}) collective-permute-start(f32[2]{0:T(128)S(1)} %broadcast_select_fusion.6), channel_id=1, source_target_pairs={{0,64},{16,80},{32,96},{48,112},{64,0},{80,16},{96,32},{112,48},{1... | collective-permute-start | bytes 32 | tf_op jit(solution)/shard_map/ppermute | solution.py:14
  141.0 12.2 %collective-permute-start.8 = (f32[2,6,9216]{2,0,1:T(2,128)S(1)}, f32[2,6,9216]{2,0,1:T(2,128)S(1)}, u32[]{:S(2)}, u32[]{:S(2)}) collective-permute-start(f32[2,6,9216]{2,0,1:T(2,128)S(1)} %broadcast_select_fusion.2), channel_id=1, source_target_pairs={{0,64},{16,80},{32,96},{48,112},{64,0},{80,16},{96,32},{112,48},{1... | collective-permute-start | bytes 1327112 | tf_op jit(solution)/shard_map/ppermute | solution.py:14
where the time goes:
time: 155 us
  waiting for transfers between devices  81.8 us (53%)
  starting transfers between devices  30 us (19%)
  local copies, waits for them, and re-layouts  16.8 us (11%)
  matrix products  15.4 us (10%)
  other arithmetic  8.35 us (5%)
  between operations  2.18 us (1%)
    ppermute x9, waiting for transfers between devices, swapped(): return lax.ppermute(value, axis, pairs)  57.1 us
    ppermute x9, starting transfers between devices, swapped(): return lax.ppermute(value, axis, pairs)  15.5 us
    dot_general x6, matrix products, contract(): jnp.einsum(form, left, right, precision=lax.Precision.HIGHEST, preferred_...  15.4 us
    all_to_all x1, waiting for transfers between devices, packed_potential(): lax.all_to_all(line_work(lax.all_to_all(spread, 'slab', split_axis=2, con...  14.1 us
    all_to_all x1, waiting for transfers between devices, packed_potential(): lax.all_to_all(spread, 'slab', split_axis=2, concat_axis=3, tiled=True)  10.6 us
    all_to_all x1, starting transfers between devices, packed_potential(): lax.all_to_all(spread, 'slab', split_axis=2, concat_axis=3, tiled=True)  7.42 us
    all_to_all x1, starting transfers between devices, packed_potential(): lax.all_to_all(line_work(lax.all_to_all(spread, 'slab', split_axis=2, con...  7.05 us
    dynamic_update_slice x2, local copies, waits for them, and re-layouts, add_returned(): lax.dynamic_update_slice_in_dim(returned, current + term[:, None], parity...  4.88 us
  transfers between devices with their start and end apart: 11, of which 9 were waited for; matrix products, arithmetic and copies ran while one was open for 6% of the time, Pallas kernels for 0%

commit v1 on v0

--- a/solution.py
+++ b/solution.py
@@ -8,10 +8,14 @@
 G = 96
 
 
-def swapped(value, axis, apart):
-    mask = 2**apart
-    pairs = [(source, source ^ mask) for source in range(lax.axis_size(axis))]
-    return lax.ppermute(value, axis, pairs)
+def partner_swap(value, pair_bits):
+    count = lax.axis_size("grp")
+
+    def direct(mask):
+        pairs = [(source, source ^ mask) for source in range(count)]
+        return lambda v: lax.ppermute(v, "grp", pairs)
+
+    return lax.switch(pair_bits - 1, [direct(mask) for mask in range(1, count)], value)
 
 
 def dft_tables(size_in, size_out, period):
@@ -23,7 +27,7 @@
 
 def contract(form, left, right):
     return jnp.einsum(
-        form, left, right, precision=lax.Precision.HIGHEST, preferred_element_type=jnp.float32
+        form, left, right, precision=lax.Precision.HIGH, preferred_element_type=jnp.float32
     )
 
 
@@ -64,14 +68,7 @@
     partner_group = jnp.bitwise_xor(own_group, pair_bits)
     upper_side = (own_group > partner_group).astype(jnp.int32)
     weights = 0.25 * occupation.astype(jnp.float32)
-    level_count = lax.axis_size("grp").bit_length() - 1
-    theirs = orbitals
-    their_weights = weights
-    for bit_level in range(level_count):
-        arrived = swapped((theirs, their_weights), "grp", bit_level)
-        chosen_flag = jnp.bitwise_and(jnp.right_shift(pair_bits, bit_level), 1) == 1
-        theirs = jnp.where(chosen_flag, arrived[0], theirs)
-        their_weights = jnp.where(chosen_flag, arrived[1], their_weights)
+    theirs, their_weights = partner_swap((orbitals, weights), pair_bits)
     paired = theirs.reshape(half_count, 2, plane_count, grid_len * grid_len)
     paired_weights = their_weights.reshape(half_count, 2)
 
@@ -118,11 +115,7 @@
     returned_start = jnp.zeros((half_count, 2, plane_count, grid_len * grid_len), jnp.float32)
     kept_rows, returned = lax.fori_loop(0, half_count, twin_step, (kept_start, returned_start))
     outgoing = returned.reshape(orbit_count, plane_count, grid_len * grid_len)
-    incoming = outgoing
-    for bit_level in range(level_count):
-        arrived_terms = swapped(incoming, "grp", bit_level)
-        chosen_flag = jnp.bitwise_and(jnp.right_shift(pair_bits, bit_level), 1) == 1
-        incoming = jnp.where(chosen_flag, arrived_terms, incoming)
+    incoming = partner_swap(outgoing, pair_bits)
     return kept_rows + incoming
 
 

time: 155 us -> 106 us (0.68)
  the two profiles are of different devices: /device:TPU:6 before, /device:TPU:1 now
where the time goes in v1:
time: 106 us; the launch traced here: 105 us
  waiting for transfers between devices  48.7 us (46%)
  local copies, waits for them, and re-layouts  18.1 us (17%)
  starting transfers between devices  16.6 us (16%)
  other arithmetic  11.4 us (11%)
  matrix products  8.17 us (8%)
  between operations  2.13 us (2%)
    ppermute x3, waiting for transfers between devices, direct(): return lambda v: lax.ppermute(v, 'grp', pairs)  19.8 us
    all_to_all x1, waiting for transfers between devices, packed_potential(): lax.all_to_all(line_work(lax.all_to_all(spread, 'slab', split_axis=2, con...  15.6 us
    all_to_all x1, waiting for transfers between devices, packed_potential(): lax.all_to_all(spread, 'slab', split_axis=2, concat_axis=3, tiled=True)  13.3 us
    all_to_all x1, starting transfers between devices, packed_potential(): lax.all_to_all(spread, 'slab', split_axis=2, concat_axis=3, tiled=True)  8.28 us
    dot_general x6, matrix products, contract(): jnp.einsum(form, left, right, precision=lax.Precision.HIGH, preferred_ele...  8.17 us
    dynamic_update_slice x2, local copies, waits for them, and re-layouts, add_returned(): lax.dynamic_update_slice_in_dim(returned, current + term[:, None], parity...  4.88 us
    mul x2, local copies, waits for them, and re-layouts, line_work(): spectra = spectra * kernel_cube[None, None]  4.46 us
    all_to_all x1, starting transfers between devices, packed_potential(): lax.all_to_all(line_work(lax.all_to_all(spread, 'slab', split_axis=2, con...  4.27 us
  transfers between devices with their start and end apart: 5, of which 4 were waited for; matrix products, arithmetic and copies ran while one was open for 7% of the time, Pallas kernels for 0%

profile of v1, /device:TPU:1, one launch (start us, length us, event | category | flops | bytes accessed | tf_op | source)
XLA Modules:
  0.0 105.2 jit_solution(16307488398553189045)
XLA Ops:
  1.5 0.7 convert_multiply_fusion
  2.2 12.7 %conditional.2 = (f32[2,6,9216]{2,0,1:T(2,128)}, f32[2]{0:T(128)}) conditional(s32[]{:T(128)} %clamp.4, (f32[2,6,9216]{2,0,1:T(2,128)}, f32[2]{0:T(128)S(1)}) %tuple.56, (f32[2,6,9216]{2,0,1:T(2,128)}, f32[2]{0:T(128)S(1)}) %tuple.56, (f32[2,6,9216]{2,0,1:T(2,128)}, f32[2]{0:T(128)S(1)}) %tuple.56, ...), branch_computations={%region_0.1_spmd, %region_1.2_spmd, %region_2.3_spmd, %region_3.4_... | conditional | bytes 1769600 | solution.py:18
  2.2 2.5 %collective-permute-start.2 = (f32[2,6,9216]{2,0,1:T(2,128)}, f32[2,6,9216]{2,0,1:T(2,128)}, u32[]{:S(2)}, u32[]{:S(2)}) collective-permute-start(f32[2,6,9216]{2,0,1:T(2,128)} %get-tuple-element.86), channel_id=1, source_target_pairs={{0,32},{16,48},{32,0},{48,16},{64,96},{80,112},{96,64},{112,80},{1... | collective-permute-start | bytes 1327112 | tf_op jit(solution)/shard_map/cond/branch_1_fun/ppermute | solution.py:16
  4.6 10.2 %collective-permute-done.3 = f32[2]{0:T(128)} collective-permute-done((f32[2]{0:T(128)S(1)}, f32[2]{0:T(128)}, u32[]{:S(2)}, u32[]{:S(2)}) %collective-permute-start.3) | collective-permute-done | bytes 40 | tf_op jit(solution)/shard_map/cond/branch_1_fun/ppermute | solution.py:16
  14.8 2.9 %multiply_reduce_fusion.1 = (f32[6,9216]{1,0:T(8,128)S(1)}, f32[6,9216]{1,0:T(8,128)S(1)}) fusion(f32[2,6,9216]{2,0,1:T(2,128)} %param.18, f32[2,6,9216]{2,0,1:T(2,128)} %get-tuple-element.101, s32[]{:T(128)S(6)} %select_n.91, s32[]{:T(128)S(6)} %select_n.94), kind=kLoop, calls=%fused_computation.41 | loop fusion | flops 110592 | bytes 1327112 | tf_op jit(solution)/shard_map/while/body/eval_jaxpr/mul | solution.py:94
  18.1 0.7 copy-done.1
  18.8 0.7 convolution_bitcast_fusion
  19.4 1.9 %copy.80 = f32[1,2,192,6,96]{4,1,3,0,2:T(2,128)} copy(f32[1,2,192,6,96]{4,2,3,1,0:T(8,128)S(1)} %convolution_bitcast_fusion) | data formatting | bytes 1769472 | tf_op jit(solution)/shard_map/while/body/eval_jaxpr/ncxyz,cdzk->ndkxy/transpose | solution.py:29
  21.4 8.3 %all-to-all-start = ((f32[1,2,192,6,96]{4,1,3,0,2:T(2,128)}), f32[1,2,192,6,96]{4,1,3,0,2:T(2,128)S(1)}, u32[]{:S(2)}, u32[]{:S(2)}) async-start(f32[1,2,192,6,96]{4,1,3,0,2:T(2,128)} %copy.80), calls=%async_computation | async-start | bytes 2359296 | tf_op jit(solution)/shard_map/while/body/eval_jaxpr/all_to_all | solution.py:58
  29.7 2.3 %mul.246 = f32[12,192,192]{2,1,0:T(8,128)S(1)} reshape(f32[12,36864]{1,0:T(8,128)} %param.20) | data formatting | bytes 3538944 | tf_op jit(solution)/shard_map/while/body/eval_jaxpr/mul | solution.py:51
  32.0 2.1 %copy.84 = f32[12,192,192]{1,2,0:T(8,128)} copy(f32[12,192,192]{2,1,0:T(8,128)S(1)} %mul.246) | data formatting | bytes 3538944 | tf_op jit(solution)/shard_map/while/body/eval_jaxpr/mul | solution.py:51
  35.0 13.3 %all-to-all-done = f32[1,2,192,6,96]{4,1,3,0,2:T(2,128)S(1)} async-done(((f32[1,2,192,6,96]{4,1,3,0,2:T(2,128)}), f32[1,2,192,6,96]{4,1,3,0,2:T(2,128)S(1)}, u32[]{:S(2)}, u32[]{:S(2)}) %all-to-all-start) | async-done | bytes 884768 | tf_op jit(solution)/shard_map/while/body/eval_jaxpr/all_to_all | solution.py:58
  48.3 0.5 copy.81
  48.9 1.1 %fusion.12 = f32[2,192,12,96,1]{3,1,4,2,0:T(8,128)S(1)} fusion(f32[2,12,96,96]{3,0,2,1:T(2,128)S(1)} %bitcast.165, f32[1,2,96,192]{2,3,0,1:T(8,128)S(1)} %copy-done.4, f32[1,2,96,192]{2,3,0,1:T(8,128)S(1)} %copy-done.2), kind=kOutput, calls=%fused_computation.12 | convolution fusion | flops 509681664 | bytes 2949120 | tf_op jit(solution)/shard_map/while/body/eval_jaxpr/nckxy,cdyl->ndkxl/dot_general | solution.py:29
  50.1 2.1 %fusion.5 = f32[2,192,12,192,1]{3,1,2,4,0:T(8,128)S(1)} fusion(f32[2,192,12,96,1]{3,1,4,2,0:T(8,128)S(1)} %fusion.12, f32[1,2,96,192]{2,3,0,1:T(8,128)S(1)} %copy-done.4, f32[1,2,96,192]{2,3,0,1:T(8,128)S(1)} %copy-done.2), kind=kOutput, calls=%fused_computation.5 | convolution fusion | flops 1019289600 | bytes 5603328 | tf_op jit(solution)/shard_map/while/body/eval_jaxpr/nckxl,cdxm->ndklm/dot_general | solution.py:29
  52.1 2.2 %fusion.1 = f32[2,96,12,192,1]{3,1,2,4,0:T(8,128)S(1)} fusion(f32[2,192,12,192,1]{3,1,2,4,0:T(8,128)S(1)} %fusion.5, f32[12,192,192]{1,2,0:T(8,128)S(1)} %copy-done, f32[1,2,192,96]{2,3,0,1:T(8,128)S(1)} %get-tuple-element.135, f32[1,2,192,96]{2,3,0,1:T(8,128)S(1)} %get-tuple-element.134), kind=kOutput, calls=%fused_computation.2 | convolution fusion | flops 1020174336 | bytes 7372800 | tf_op jit(solution)/shard_map/while/body/eval_jaxpr/ncklm,cdmx->ndklx/dot_general | solution.py:29
  54.3 1.4 %fusion.8 = f32[1,2,12,96,96]{3,4,2,1,0:T(8,128)S(1)} fusion(f32[2,96,12,192,1]{3,1,2,4,0:T(8,128)S(1)} %fusion.1, f32[1,2,192,96]{2,3,0,1:T(8,128)S(1)} %get-tuple-element.135, f32[1,2,192,96]{2,3,0,1:T(8,128)S(1)} %get-tuple-element.134), kind=kOutput, calls=%fused_computation.8 | convolution fusion | flops 509681664 | bytes 2949120 | tf_op jit(solution)/shard_map/while/body/eval_jaxpr/ncklx,cdly->ndkxy/dot_general | solution.py:29
  55.7 1.4 %copy.87 = f32[1,2,12,96,96]{4,1,2,0,3:T(2,128)} copy(f32[1,2,12,96,96]{3,4,2,1,0:T(8,128)S(1)} %fusion.8) | data formatting | bytes 1769472 | tf_op jit(solution)/shard_map/while/body/eval_jaxpr/ncklx,cdly->ndkxy/transpose | solution.py:29
  57.2 4.3 %all-to-all-start.1 = ((f32[1,2,12,96,96]{4,1,2,0,3:T(2,128)}), f32[1,2,12,96,96]{4,1,2,0,3:T(2,128)S(1)}, u32[]{:S(2)}, u32[]{:S(2)}) async-start(f32[1,2,12,96,96]{4,1,2,0,3:T(2,128)} %copy.87), calls=%async_computation.1 | async-start | bytes 2359296 | tf_op jit(solution)/shard_map/while/body/eval_jaxpr/all_to_all | solution.py:57
  61.4 0.6 fusion.48
  63.2 1.3 %fusion.47 = (f32[1]{0:T(128)}, f32[1]{0:T(128)}) fusion(f32[2]{0:T(128)} %get-tuple-element.100, s32[]{:T(128)S(6)} %select_n.91, s32[]{:T(128)S(6)} %select_n.94), kind=kLoop, calls=%fused_computation.73 | loop fusion | bytes 24 | tf_op jit(solution)/shard_map/dynamic-slice
  64.6 15.6 %all-to-all-done.1 = f32[1,2,12,96,96]{4,1,2,0,3:T(2,128)S(1)} async-done(((f32[1,2,12,96,96]{4,1,2,0,3:T(2,128)}), f32[1,2,12,96,96]{4,1,2,0,3:T(2,128)S(1)}, u32[]{:S(2)}, u32[]{:S(2)}) %all-to-all-start.1) | async-done | bytes 884768 | tf_op jit(solution)/shard_map/while/body/eval_jaxpr/all_to_all | solution.py:57
  80.2 0.5 copy.88
  81.2 0.7 convolution_bitcast_fusion.1
  82.1 0.6 reshape.249
  83.5 0.5 fusion.24
  84.0 4.7 %dynamic_update_slice.25 = f32[2,6,9216]{2,0,1:T(2,128)S(1)} dynamic-update-slice(f32[2,6,9216]{2,0,1:T(2,128)S(1)} %bitcast.167, f32[1,6,9216]{2,0,1:T(1,128)S(1)} %fusion.24, s32[]{:T(128)S(6)} %select_n.94, s32[]{:T(128)} %constant.84.clone.1, s32[]{:T(128)} %constant.84.clone.1) | dynamic-update-slice | bytes 442372 | tf_op jit(solution)/shard_map/while/body/eval_jaxpr/dynamic_update_slice | solution.py:77
  88.6 11.2 %conditional.3 = (f32[2,6,9216]{2,0,1:T(2,128)}) conditional(s32[]{:T(128)} %clamp.4, f32[2,6,9216]{2,0,1:T(2,128)S(1)} %dynamic_update_slice.25, f32[2,6,9216]{2,0,1:T(2,128)S(1)} %dynamic_update_slice.25, f32[2,6,9216]{2,0,1:T(2,128)S(1)} %dynamic_update_slice.25, ...), branch_computations={%region_7.8_spmd, %region_8.9_spmd, %region_9.10_spmd, %region_10.... | conditional | bytes 1769520 | solution.py:18
  88.7 1.5 %collective-permute-start.15 = (f32[2,6,9216]{2,0,1:T(2,128)S(1)}, f32[2,6,9216]{2,0,1:T(2,128)}, u32[]{:S(2)}, u32[]{:S(2)}) collective-permute-start(f32[2,6,9216]{2,0,1:T(2,128)S(1)} %param.8), channel_id=1, source_target_pairs={{0,32},{16,48},{32,0},{48,16},{64,96},{80,112},{96,64},{112,80},{1... | collective-permute-start | bytes 1327112 | tf_op jit(solution)/shard_map/cond/branch_1_fun/ppermute | solution.py:16
  90.2 9.6 %collective-permute-done.15 = f32[2,6,9216]{2,0,1:T(2,128)} collective-permute-done((f32[2,6,9216]{2,0,1:T(2,128)S(1)}, f32[2,6,9216]{2,0,1:T(2,128)}, u32[]{:S(2)}, u32[]{:S(2)}) %collective-permute-start.15) | collective-permute-done | bytes 442400 | tf_op jit(solution)/shard_map/cond/branch_1_fun/ppermute | solution.py:16
  99.8 3.1 %fusion.26 = (f32[1,6,9216]{2,0,1:T(1,128)S(1)}, f32[1,6,9216]{2,0,1:T(1,128)S(1)}) fusion(f32[1,2,6,9216]{3,1,2,0:T(2,128)S(1)} %reshape.249, f32[2,6,9216]{2,0,1:T(2,128)} %get-tuple-element.101, s32[]{:T(128)S(6)} %select_n.91, f32[]{:T(128)} %bitcast.1, s32[]{:T(128)S(6)} %select_n.94, f32[]{:T(128)} %bitcast.55), kind=kLoop, calls=%fused_computation.39 | loop fusion | flops 331776 | bytes 1327120 | tf_op jit(solution)/shard_map/while/body/eval_jaxpr/neg | solution.py:102
  102.9 2.3 %maximum_add_fusion = f32[2,6,9216]{2,0,1:T(2,128)} fusion(f32[2,6,9216]{2,0,1:T(2,128)} %get-tuple-element.160, f32[1,6,9216]{2,0,1:T(1,128)S(1)} %get-tuple-element.133, f32[1,6,9216]{2,0,1:T(1,128)S(1)} %get-tuple-element.132), kind=kLoop, calls=%fused_computation.19 | loop fusion | flops 221184 | bytes 1327104 | tf_op jit(solution)/shard_map/add | solution.py:119
  (26 shorter events, 3.4 us)
Async XLA Ops:
  2.2 12.7 %collective-permute-start.2 = (f32[2,6,9216]{2,0,1:T(2,128)}, f32[2,6,9216]{2,0,1:T(2,128)}, u32[]{:S(2)}, u32[]{:S(2)}) collective-permute-start(f32[2,6,9216]{2,0,1:T(2,128)} %get-tuple-element.86), channel_id=1, source_target_pairs={{0,32},{16,48},{32,0},{48,16},{64,96},{80,112},{96,64},{112,80},{1... | collective-permute-start | bytes 1327112 | tf_op jit(solution)/shard_map/cond/branch_1_fun/ppermute | solution.py:16
  4.6 10.2 %collective-permute-start.3 = (f32[2]{0:T(128)S(1)}, f32[2]{0:T(128)}, u32[]{:S(2)}, u32[]{:S(2)}) collective-permute-start(f32[2]{0:T(128)S(1)} %get-tuple-element.87), channel_id=1, source_target_pairs={{0,32},{16,48},{32,0},{48,16},{64,96},{80,112},{96,64},{112,80},{1... | collective-permute-start | bytes 32 | tf_op jit(solution)/shard_map/cond/branch_1_fun/ppermute | solution.py:16
  18.0 0.7 copy-start.1
  18.0 0.7 copy-start.3
  21.4 26.9 %all-to-all-start = ((f32[1,2,192,6,96]{4,1,3,0,2:T(2,128)}), f32[1,2,192,6,96]{4,1,3,0,2:T(2,128)S(1)}, u32[]{:S(2)}, u32[]{:S(2)}) async-start(f32[1,2,192,6,96]{4,1,3,0,2:T(2,128)} %copy.80), calls=%async_computation | async-start | bytes 2359296 | tf_op jit(solution)/shard_map/while/body/eval_jaxpr/all_to_all | solution.py:58
  34.1 14.8 %copy-start.2 = (f32[1,2,96,192]{2,3,0,1:T(8,128)S(1)}, f32[1,2,96,192]{2,3,0,1:T(8,128)}, u32[]{:S(2)}) copy-start(f32[1,2,96,192]{2,3,0,1:T(8,128)} %copy-done.1) | copy-start | bytes 442372
  34.1 14.8 %copy-start.4 = (f32[1,2,96,192]{2,3,0,1:T(8,128)S(1)}, f32[1,2,96,192]{2,3,0,1:T(8,128)}, u32[]{:S(2)}) copy-start(f32[1,2,96,192]{2,3,0,1:T(8,128)} %copy-done.3) | copy-start | bytes 442372
  50.0 2.1 %copy-start = (f32[12,192,192]{1,2,0:T(8,128)S(1)}, f32[12,192,192]{1,2,0:T(8,128)}, u32[]{:S(2)}) copy-start(f32[12,192,192]{1,2,0:T(8,128)} %copy.84) | copy-start | bytes 5308420
  57.2 23.0 %all-to-all-start.1 = ((f32[1,2,12,96,96]{4,1,2,0,3:T(2,128)}), f32[1,2,12,96,96]{4,1,2,0,3:T(2,128)S(1)}, u32[]{:S(2)}, u32[]{:S(2)}) async-start(f32[1,2,12,96,96]{4,1,2,0,3:T(2,128)} %copy.87), calls=%async_computation.1 | async-start | bytes 2359296 | tf_op jit(solution)/shard_map/while/body/eval_jaxpr/all_to_all | solution.py:57
  81.2 1.8 %copy-start.5 = (f32[2,6,9216]{2,0,1:T(2,128)S(1)}, f32[2,6,9216]{2,0,1:T(2,128)}, u32[]{:S(2)}) copy-start(f32[2,6,9216]{2,0,1:T(2,128)} %param.18) | copy-start | bytes 1327108
  88.7 11.1 %collective-permute-start.15 = (f32[2,6,9216]{2,0,1:T(2,128)S(1)}, f32[2,6,9216]{2,0,1:T(2,128)}, u32[]{:S(2)}, u32[]{:S(2)}) collective-permute-start(f32[2,6,9216]{2,0,1:T(2,128)S(1)} %param.8), channel_id=1, source_target_pairs={{0,32},{16,48},{32,0},{48,16},{64,96},{80,112},{96,64},{112,80},{1... | collective-permute-start | bytes 1327112 | tf_op jit(solution)/shard_map/cond/branch_1_fun/ppermute | solution.py:16
